TPU v7x, 32 devices: a whole 2x2x4 slice. The times are simulated.
32 devices in a mesh: tm: 8 (over y, x, core), cell: 4 (over z).
Axes of the slice: x: 2, y: 2, z: 4, core: 2. Of those that a mesh axis runs over, the one named last changes fastest.
Arguments:
- anomalies: bfloat16 [24, 2, 8192, 256], P('tm', None, 'cell'), may hold values from -6 to 6
- obs_cells: int32 [24, 128], P('tm', 'cell'), may hold values from 0 to 8191, as said below
- obs_counts: int32 [24, 4], P('tm', 'cell'), may hold values from 16 to 32
- obs_precision: float32 [24, 128], P('tm', 'cell'), may hold values from 0.1 to 1
- inflation: float32 [24], P('tm'), may hold values from 1 to 1.12
Outputs:
- smoothed: bfloat16 [24, 2, 8192, 256], P('tm', None, 'cell')
Inputs may be any that keep to these rules, and one draw needn't show every extreme that they name: `obs_cells`: slot k of a window names a cell of the block of 2048 cells that starts at (k // 32) * 2048; two slots may name the same cell.
All inputs are finite; a program needn't handle non-finite values.
Results may differ from a plain program's by a relative error of at most 0.017.
Values may be sent and summed in bfloat16 or wider, within the bound.
A program may use at most 128 MiB of HBM per device.

v0:
```python
import jax
import jax.numpy as jnp
from jax import lax
from jax.sharding import PartitionSpec as P


def matmul_f32(left, right):
    return jnp.dot(left, right, precision=lax.Precision.HIGHEST, preferred_element_type=jnp.float32)


def gram_of(picked, weights):
    as_float = picked.astype(jnp.float32)
    weighted = as_float * weights[:, :, None]
    return jnp.einsum(
        "wkm,wkn->wmn",
        weighted,
        as_float,
        precision=lax.Precision.HIGHEST,
        preferred_element_type=jnp.float32,
    )


def transform_of(gram, rho):
    members = gram.shape[-1]
    unit_matrix = jnp.eye(members, dtype=jnp.float32)
    factor = jnp.linalg.cholesky((members - 1.0) * unit_matrix[None] + gram)
    inverse = jax.vmap(
        lambda lower_f: jax.scipy.linalg.solve_triangular(lower_f, unit_matrix, lower=True)
    )(factor)
    scale = rho * jnp.sqrt(jnp.float32(members - 1.0))
    return scale[:, None, None] * jnp.swapaxes(inverse, 1, 2)


def local(anomalies, obs_cells, obs_counts, obs_precision, inflation):
    cell_width = anomalies.shape[2]
    members = anomalies.shape[3]
    slots = obs_cells.shape[1]
    first_cell = lax.axis_index("cell") * cell_width
    offsets = obs_cells - first_cell
    picked = jax.vmap(lambda field, where_at: field[0][where_at])(anomalies, offsets)
    live = jnp.arange(slots, dtype=jnp.int32)[None, :] < obs_counts
    picked = jnp.where(live[:, :, None], picked, jnp.zeros_like(picked))
    weights = jnp.where(live, obs_precision, jnp.float32(0.0))
    gathered, gathered_weights = (
        lax.all_gather(picked, "cell", axis=1, tiled=True),
        lax.all_gather(weights.astype(jnp.bfloat16), "cell", axis=1, tiled=True).astype(
            weights.dtype
        ),
    )
    gram = gram_of(gathered, gathered_weights)
    transforms = transform_of(gram, inflation)
    windows = transforms.shape[0]
    partial_list = [transforms[windows - 1]]
    for window in range(windows - 2, -1, -1):
        partial_list.insert(0, matmul_f32(transforms[window], partial_list[0]))
    own_product = partial_list[0]
    unit_matrix = jnp.eye(members, dtype=jnp.float32)
    products = lax.all_gather(
        own_product[None].astype(jnp.bfloat16), "tm", axis=0, tiled=True
    ).astype(jnp.float32)
    count = lax.axis_size("tm")
    position = lax.axis_index("tm")

    def absorb(turn, carried):
        source = count - 1 - turn
        updated = matmul_f32(products[source], carried)
        return jnp.where(source > position, updated, carried)

    later_product = lax.fori_loop(0, count, absorb, unit_matrix)
    suffixes = jnp.stack(
        [matmul_f32(partial_value, later_product) for partial_value in partial_list]
    )
    weight_mats = suffixes.astype(jnp.bfloat16)
    flat = anomalies.reshape(windows, 2 * cell_width, members)
    result = jnp.einsum("wcm,wmn->wcn", flat, weight_mats, preferred_element_type=jnp.float32)
    return result.astype(jnp.bfloat16).reshape(anomalies.shape)


def solution(mesh):
    placed = (
        P("tm", None, "cell", None),
        P("tm", "cell"),
        P("tm", "cell"),
        P("tm", "cell"),
        P("tm"),
    )
    return jax.shard_map(
        local, mesh=mesh, in_specs=placed, out_specs=P("tm", None, "cell", None), check_vma=False
    )
```

profile of v0, /device:TPU:0, one launch (start us, length us, event | category | flops | bytes accessed | tf_op | source)
XLA Modules:
  0.0 269.0 jit_solution(16111272196419085937)
XLA Ops:
  6.5 0.5 iota_multiply_fusion
  7.0 0.6 iota_compare_fusion.4
  7.7 0.6 iota_compare_fusion.3
  8.3 0.6 iota_compare_fusion.2
  8.9 0.8 fusion.21
  9.8 0.7 iota_compare_fusion.5
  10.5 0.7 broadcast_multiply_fusion
  11.2 0.8 fusion.35
  11.9 0.7 fusion.34
  12.7 12.6 %all-gather.1 = bf16[4,32,3]{1,2,0:T(4,128)(2,1)S(1)} all-gather(bf16[1,32,3]{1,2,0:T(4,128)(2,1)S(1)} %fusion.35), channel_id=1, replica_groups=mesh['tm'=8,'cell'=4] {'cell'}, dimensions={0}, use_global_device_ids=true | all-gather | bytes 960 | tf_op jit(solution)/shard_map/all_gather | solution.py:46
  25.4 0.7 fusion.38
  26.1 2.1 slice_bitcast_fusion
  28.2 2.2 gather_fusion
  30.4 0.9 broadcast_select_fusion
  31.3 13.6 %all_gather.9 = bf16[3,128,256]{2,1,0:T(8,128)(2,1)S(1)} all-gather(bf16[3,32,256]{2,1,0:T(8,128)(2,1)S(1)} %broadcast_select_fusion), channel_id=1, replica_groups=mesh['tm'=8,'cell'=4] {'cell'}, dimensions={1}, use_global_device_ids=true | all-gather | bytes 245760 | tf_op jit(solution)/shard_map/all_gather | solution.py:45
  44.9 0.6 fusion.15
  45.7 1.2 fusion.9
  46.9 35.2 %custom-call.17 = f32[3,128,128]{2,1,0:T(8,128)S(1)} custom-call(f32[3,128,128]{2,1,0:T(8,128)S(1)} %cholesky.122), custom_call_target="Cholesky" | custom-call | tf_op jit(solution)/shard_map/jit(cholesky)/cholesky | solution.py:26
  82.1 29.5 %custom-call.18 = f32[3,1,128,128]{2,3,1,0:T(8,128)S(1)} custom-call(f32[3,1,128,128]{3,2,1,0:T(8,128)S(1)} %select_bitcast_fusion), custom_call_target="InvertDiagBlocksLowerTriangular" | custom-call | tf_op jit(solution)/shard_map/jit(cholesky)/cholesky | solution.py:26
  112.1 0.5 convolution_subtract_fusion.1
  112.6 35.2 %custom-call.19 = f32[3,128,128]{2,1,0:T(8,128)S(1)} custom-call(f32[3,128,128]{2,1,0:T(8,128)S(1)} %convolution_subtract_fusion.1), custom_call_target="Cholesky" | custom-call | tf_op jit(solution)/shard_map/jit(cholesky)/cholesky | solution.py:26
  148.3 5.4 %while.17 = (s32[]{:T(128)}, f32[3,256,256]{2,1,0:T(8,128)S(1)}, s32[2,2]{1,0:T(2,128)S(1)}, f32[2,3,128,128]{3,2,0,1:T(8,128)}, s32[]{:T(128)}) while((s32[]{:T(128)}, f32[3,256,256]{2,1,0:T(8,128)S(1)}, s32[2,2]{1,0:T(2,128)S(1)}, f32[2,3,128,128]{3,2,0,1:T(8,128)}, s32[]{:T(128)}) %tuple.56), condition=%wide.while_cond, body=%wide.while_body.sunk | while | flops 2 | bytes 394349 | solution.py:28
  148.3 0.6 fusion.58
  148.9 2.1 bitcast_dynamic-update-slice_fusion.2
  151.0 0.6 fusion.58
  151.6 2.1 bitcast_dynamic-update-slice_fusion.2
  153.7 59.8 %custom-call.20 = f32[3,2,128,128]{2,3,1,0:T(8,128)S(1)} custom-call(f32[3,2,128,128]{3,2,1,0:T(8,128)} %bitcast.105), custom_call_target="InvertDiagBlocksLowerTriangular" | custom-call | tf_op jit(solution)/shard_map/vmap(jit(_solve_triangular))/triangular_solve | solution.py:28
  213.5 0.5 fusion.25
  214.1 0.5 convolution_subtract_fusion
  214.5 0.5 fusion.24
  215.2 0.6 fusion.18
  215.8 1.3 fusion.39
  217.2 21.8 %all-gather.4.cloned.1.call-done = bf16[2048,256]{1,0:T(8,128)(2,1)} async-done(((bf16[256,256]{1,0:T(8,128)(2,1)}), bf16[2048,256]{1,0:T(8,128)(2,1)}) %all-gather.4.cloned.1.call-update) | async-done | bytes 1048592 | tf_op jit(solution)/shard_map/all_gather | solution.py:58
  238.9 1.4 convert.15
  240.4 3.5 %while.16 = (s32[]{:T(128)}, f32[256,256]{1,0:T(8,128)S(1)}, s32[]{:T(128)}, f32[8,256,256]{2,1,0:T(8,128)S(1)}, s32[]{:T(128)}, /*index=5*/s32[]{:T(128)}, s32[]{:T(128)}, s32[]{:T(128)}) while((s32[]{:T(128)}, f32[256,256]{1,0:T(8,128)S(1)}, s32[]{:T(128)}, f32[8,256,256]{2,1,0:T(8,128)S(1)}, s32[]{:T(128)}, /*index=5*/s32[]{:T(128)}, ...), condition=%wide.region_5.6_spmd, body=%wide.region_4.5_spmd.sunk | while | flops 201392128 | bytes 1573017 | solution.py:69
  240.4 0.4 convolution_select_fusion.2
  240.9 0.4 convolution_select_fusion.2
  241.3 0.4 convolution_select_fusion.2
  241.7 0.4 convolution_select_fusion.2
  242.2 0.4 convolution_select_fusion.2
  242.6 0.4 convolution_select_fusion.2
  243.1 0.4 convolution_select_fusion.2
  243.5 0.4 convolution_select_fusion.2
  243.9 0.6 fusion.6
  244.5 0.4 fusion.5
  244.9 1.3 fusion.4
  246.2 7.3 %fusion.3 = bf16[3,4096,256]{1,2,0:T(8,128)(2,1)} fusion(bf16[3,4096,256]{2,1,0:T(8,128)(2,1)} %bitcast.99, bf16[1,256,256]{2,1,0:T(8,128)(2,1)S(1)} %fusion.6, bf16[1,256,256]{2,1,0:T(8,128)(2,1)S(1)} %fusion.5, bf16[1,256,256]{2,1,0:T(8,128)(2,1)S(1)} %fusion.4), kind=kOutput, calls=%fused_computation.8 | convolution fusion | flops 1614151680 | bytes 12976128 | tf_op jit(solution)/shard_map/wcm,wmn->wcn/dot_general | solution.py:75
  253.5 8.6 %copy.65 = bf16[3,4096,256]{2,1,0:T(8,128)(2,1)} copy(bf16[3,4096,256]{1,2,0:T(8,128)(2,1)} %fusion.3) | data formatting | bytes 12582912 | tf_op jit(solution)/shard_map/reshape | solution.py:76
  (39 shorter events, 1.8 us)
Async XLA Ops:
  6.5 232.4 %all-gather.4.cloned.1.call-start = ((), (), s32[]{:S(2)}) async-start(), calls=%async_computation | async-start | bytes 1179648 | tf_op jit(solution)/shard_map/all_gather | solution.py:58
  30.3 51.8 %copy-start.3 = (pred[128,128]{1,0:T(8,128)(4,1)S(1)}, pred[128,128]{1,0:T(8,128)(4,1)}, u32[]{:S(2)}) copy-start(pred[128,128]{1,0:T(8,128)(4,1)} %iota_compare_fusion.3) | copy-start | bytes 49156
  30.3 117.4 %copy-start.2 = (pred[128,128]{1,0:T(8,128)(4,1)S(1)}, pred[128,128]{1,0:T(8,128)(4,1)}, u32[]{:S(2)}) copy-start(pred[128,128]{1,0:T(8,128)(4,1)} %iota_compare_fusion.4) | copy-start | bytes 49156
  30.4 117.7 %copy-start.1 = (pred[256,256]{1,0:T(8,128)(4,1)S(1)}, pred[256,256]{1,0:T(8,128)(4,1)}, u32[]{:S(2)}) copy-start(pred[256,256]{1,0:T(8,128)(4,1)} %iota_compare_fusion.2) | copy-start | bytes 196612
  30.4 117.9 %copy-start.4 = (s32[2]{0:T(128)S(1)}, s32[2]{0:T(128)}, u32[]{:S(2)}) copy-start(s32[2]{0:T(128)} %iota_multiply_fusion) | copy-start | bytes 28
  45.5 168.1 %copy-start = (f32[128,256]{1,0:T(8,128)S(1)}, f32[128,256]{1,0:T(8,128)}, u32[]{:S(2)}) copy-start(f32[128,256]{1,0:T(8,128)} %get-tuple-element.145) | copy-start | bytes 393220
Sparse Core Ops, SparseCore 0:
  217.3 21.6 all-gather.3
where the time goes:
time: 270 us; the launch traced here: 269 us
  other arithmetic  170 us (63%)
  blocking collectives  26.2 us (10%)
  waiting for transfers between devices  21.8 us (8%)
  local copies, waits for them, and re-layouts  19.6 us (7%)
  matrix products  17.6 us (7%)
  between operations  13.6 us (5%)
    another operation x10, other arithmetic, transform_of(): factor = jnp.linalg.cholesky((members - 1.0) * unit_matrix[None] + gram)  101 us
    another operation x4, other arithmetic, transform_of(): jax.scipy.linalg.solve_triangular(lower_f, unit_matrix, lower=True)  61.1 us
    all_gather x1, waiting for transfers between devices, local(): lax.all_gather(own_product[None].astype(jnp.bfloat16), 'tm', axis=0, tile...  21.8 us
    all_gather x1, blocking collectives, local(): lax.all_gather(picked, 'cell', axis=1, tiled=True)  13.6 us
    all_gather x1, blocking collectives, local(): lax.all_gather(weights.astype(jnp.bfloat16), 'cell', axis=1, tiled=True)  12.6 us
    reshape x1, local copies, waits for them, and re-layouts, local(): return result.astype(jnp.bfloat16).reshape(anomalies.shape)  8.6 us
    dot_general x13, matrix products, matmul_f32(): jnp.dot(left, right, precision=lax.Precision.HIGHEST, preferred_element_t...  7.3 us
    dot_general x1, matrix products, local(): jnp.einsum('wcm,wmn->wcn', flat, weight_mats, preferred_element_type=jnp....  7.3 us
  transfers between devices with their start and end apart: 1, of which 1 were waited for; matrix products, arithmetic and copies ran while one was open for 0% of the time, Pallas kernels for 0%

commit v1 on v0

v1 whole, which is shorter than its diff:
```python
import jax
import jax.numpy as jnp
from jax import lax
from jax.experimental import pallas as pl
from jax.experimental.pallas import tpu as pltpu
from jax.sharding import PartitionSpec as P

F32 = jnp.float32
BF16 = jnp.bfloat16


def dot_any(left, right, dims):
    return lax.dot_general(left, right, (dims, ((), ())), preferred_element_type=F32)


def halves(value):
    high = value.astype(BF16)
    return high, (value - high.astype(F32)).astype(BF16)


def dot_three(left, right, dims=((1,), (0,))):
    lh, ll = halves(left)
    rh, rl = halves(right)
    return dot_any(lh, rh, dims) + (dot_any(lh, rl, dims) + dot_any(ll, rh, dims))


def dot_full(left, right, dims=((1,), (0,))):
    return lax.dot_general(
        left, right, (dims, ((), ())), precision=lax.Precision.HIGHEST, preferred_element_type=F32
    )


def eliminate(matrices):
    size = matrices[0].shape[0]
    groups = size // 8
    lane = lax.broadcasted_iota(jnp.int32, (8, size), 1)
    sub = lax.broadcasted_iota(jnp.int32, (8, size), 0)
    work = [[m[8 * g : 8 * g + 8, :] for g in range(groups)] for m in matrices]
    for k in range(size):
        g, r = divmod(k, 8)
        at_k = lane == k
        below = sub > r
        for rows in work:
            own = rows[g]
            pivot_row = jnp.broadcast_to(own[r : r + 1, :], (8, size))
            inverse = 1.0 / own[r : r + 1, k : k + 1]
            scaled = jnp.where(at_k, 1.0, pivot_row) * inverse
            for i in range(g, groups):
                column = jnp.broadcast_to(rows[i][:, k : k + 1], (8, size))
                if i == g:
                    if r == 7:
                        continue
                    column = jnp.where(below, column, 0.0)
                    base = jnp.where(at_k & below, 0.0, rows[i])
                else:
                    base = jnp.where(at_k, 0.0, rows[i])
                rows[i] = base - column * scaled
    results = []
    for rows in work:
        pieces = []
        for g in range(groups):
            row = sub + 8 * g
            pivot = jnp.sum(jnp.where(lane == row, rows[g], 0.0), axis=1, keepdims=True)
            unit = jnp.where(lane < row, rows[g], jnp.where(lane == row, 1.0, 0.0))
            pieces.append(unit * lax.rsqrt(pivot))
        results.append(jnp.concatenate(pieces, axis=0))
    return results


def transforms_kernel(
    rho_ref, picked_ref, weight_ref, partial_ref, own_ref, gram, first_inv, second_inv, low_ref, mid_ref
):
    windows = picked_ref.shape[0]
    members = picked_ref.shape[2]
    half = members // 2
    eye = (
        lax.broadcasted_iota(jnp.int32, (members, members), 0)
        == lax.broadcasted_iota(jnp.int32, (members, members), 1)
    )
    tn = ((0,), (0,))
    nt = ((1,), (1,))

    @pl.loop(0, windows)
    def _(w):
        rows = picked_ref[w]
        high, low = halves(rows.astype(F32) * weight_ref[w])
        total = dot_any(high, rows, tn) + dot_any(low, rows, tn)
        gram[w] = total + jnp.where(eye, F32(members - 1.0), 0.0)

    for w, value in enumerate(eliminate([gram[w, :half, :half] for w in range(windows)])):
        first_inv[w] = value

    @pl.loop(0, windows)
    def _(w):
        lower = dot_full(gram[w, half:, :half], first_inv[w], nt)
        low_ref[w] = lower
        gram[w, half:, half:] -= dot_full(lower, lower, nt)
        mid_ref[w] = dot_full(lower, first_inv[w])

    for w, value in enumerate(eliminate([gram[w, half:, half:] for w in range(windows)])):
        second_inv[w] = value

    zero = jnp.zeros((half, half), F32)

    @pl.loop(0, windows)
    def _(w):
        scale = rho_ref[w] * jnp.sqrt(F32(members - 1.0))
        cross = -dot_full(second_inv[w], mid_ref[w])
        partial_ref[w, :half, :half] = scale * first_inv[w].T
        partial_ref[w, :half, half:] = scale * cross.T
        partial_ref[w, half:, :half] = zero
        partial_ref[w, half:, half:] = scale * second_inv[w].T

    @pl.loop(0, windows - 1)
    def _(turn):
        w = windows - 2 - turn
        partial_ref[w] = dot_three(partial_ref[w], partial_ref[w + 1])

    own_ref[0] = partial_ref[0, :half, :half].astype(BF16)
    own_ref[1] = partial_ref[0, :half, half:].astype(BF16)
    own_ref[2] = partial_ref[0, half:, half:].astype(BF16)


def fold_kernel(position_ref, products_ref, partial_ref, out_ref, whole, later):
    count = products_ref.shape[0]
    windows, members, _ = partial_ref.shape
    half = members // 2
    position = position_ref[0]
    whole[...] = jnp.zeros_like(whole)
    later[...] = (
        lax.broadcasted_iota(jnp.int32, (members, members), 0)
        == lax.broadcasted_iota(jnp.int32, (members, members), 1)
    ).astype(F32)

    @pl.loop(0, count - 1 - position)
    def _(turn):
        source = count - 1 - turn
        whole[:half, :half] = products_ref[source, 0]
        whole[:half, half:] = products_ref[source, 1]
        whole[half:, half:] = products_ref[source, 2]
        high, low = halves(later[...])
        left = whole[...]
        later[...] = dot_any(left, high, ((1,), (0,))) + dot_any(left, low, ((1,), (0,)))

    @pl.loop(0, windows)
    def _(w):
        out_ref[w] = dot_three(partial_ref[w], later[...]).astype(BF16)


def local(anomalies, obs_cells, obs_counts, obs_precision, inflation):
    windows, _, cell_width, members = anomalies.shape
    half = members // 2
    slots = obs_cells.shape[1]
    first_cell = lax.axis_index("cell") * cell_width
    offsets = obs_cells - first_cell
    picked = jax.vmap(lambda field, where_at: field[0][where_at])(anomalies, offsets)
    live = jnp.arange(slots, dtype=jnp.int32)[None, :] < obs_counts
    weights = jnp.where(live, obs_precision, jnp.float32(0.0))
    gathered = lax.all_gather(picked, "cell", axis=1, tiled=True)
    gathered_weights = lax.all_gather(weights, "cell", axis=1, tiled=True)
    vmem = pl.BlockSpec(memory_space=pltpu.VMEM)
    smem = pl.BlockSpec(memory_space=pltpu.SMEM)
    partial, own = pl.pallas_call(
        transforms_kernel,
        out_shape=(
            jax.ShapeDtypeStruct((windows, members, members), F32),
            jax.ShapeDtypeStruct((3, half, half), BF16),
        ),
        in_specs=[smem, vmem, vmem],
        out_specs=(vmem, vmem),
        scratch_shapes=[pltpu.VMEM((windows, members, members), F32)]
        + [pltpu.VMEM((windows, half, half), F32)] * 4,
        name="transforms",
    )(inflation, gathered, gathered_weights[:, :, None])
    products = lax.all_gather(own, "tm", axis=0)
    weight_mats = pl.pallas_call(
        fold_kernel,
        out_shape=jax.ShapeDtypeStruct((windows, members, members), BF16),
        in_specs=[smem, vmem, vmem],
        out_specs=vmem,
        scratch_shapes=[pltpu.VMEM((members, members), BF16), pltpu.VMEM((members, members), F32)],
        name="fold",
    )(lax.axis_index("tm").astype(jnp.int32)[None], products, partial)
    flat = anomalies.reshape(windows, 2 * cell_width, members)
    result = jnp.einsum("wcm,wmn->wcn", flat, weight_mats, preferred_element_type=jnp.float32)
    return result.astype(jnp.bfloat16).reshape(anomalies.shape)


def solution(mesh):
    placed = (
        P("tm", None, "cell", None),
        P("tm", "cell"),
        P("tm", "cell"),
        P("tm", "cell"),
        P("tm"),
    )
    return jax.shard_map(
        local, mesh=mesh, in_specs=placed, out_specs=P("tm", None, "cell", None), check_vma=False
    )
```

time: 270 us -> 109 us (0.40)
  other arithmetic: 170 us -> 1.44 us
  Pallas kernels: 0 us -> 45.4 us
  waiting for transfers between devices: 21.8 us -> 0 us
  blocking collectives: 26.2 us -> 40.7 us
  between operations: 13.6 us -> 0.01 us
  matrix products: 17.6 us -> 7.44 us
  local copies, waits for them, and re-layouts: 19.6 us -> 13.2 us
    another operation x14 -> x0, other arithmetic: 162 us -> none  [the longest x10 101 us: transform_of(): factor = jnp.linalg.cholesky((members - 1.0) * unit_matrix[None] + gram)]
    pallas_call x0 -> x2, Pallas kernels: none -> 45.4 us  [the longest x1 40.8 us: local(): pl.pallas_call(transforms_kernel, out_shape=(jax.ShapeDtypeStruct((window...]
    all_gather x1 -> x0, waiting for transfers between devices: 21.8 us -> none  [local(): lax.all_gather(own_product[None].astype(jnp.bfloat16), 'tm', axis=0, tile...]
    all_gather x2 -> x3, blocking collectives: 26.2 us -> 40.7 us  [the longest x1 14.6 us: local(): gathered = lax.all_gather(picked, 'cell', axis=1, tiled=True)]
    dot_general x14 -> x0, matrix products: 7.88 us -> none  [the longest x13 7.3 us: matmul_f32(): jnp.dot(left, right, precision=lax.Precision.HIGHEST, preferred_element_t...]
    another operation x10 -> x0, local copies, waits for them, and re-layouts: 6.2 us -> none
  transfers between devices with their start and end apart: 1 -> 0, of which waited for: 1 -> 0; matrix products, arithmetic and copies ran while one was open for 0% -> 0% of each run, Pallas kernels for 0% -> 0%
where the time goes in v1:
time: 109 us; the launch traced here: 108 us
  Pallas kernels  45.4 us (42%)
  blocking collectives  40.7 us (37%)
  local copies, waits for them, and re-layouts  13.2 us (12%)
  matrix products  7.44 us (7%)
  other arithmetic  1.44 us (1%)
    pallas_call x1, Pallas kernels, local(): pl.pallas_call(transforms_kernel, out_shape=(jax.ShapeDtypeStruct((window...  40.8 us
    all_gather x1, blocking collectives, local(): gathered = lax.all_gather(picked, 'cell', axis=1, tiled=True)  14.6 us
    all_gather x1, blocking collectives, local(): gathered_weights = lax.all_gather(weights, 'cell', axis=1, tiled=True)  13.6 us
    all_gather x1, blocking collectives, local(): products = lax.all_gather(own, 'tm', axis=0)  12.5 us
    reshape x1, local copies, waits for them, and re-layouts, local(): return result.astype(jnp.bfloat16).reshape(anomalies.shape)  8.6 us
    dot_general x1, matrix products, local(): jnp.einsum('wcm,wmn->wcn', flat, weight_mats, preferred_element_type=jnp....  7.44 us
    pallas_call x1, Pallas kernels, local(): pl.pallas_call(fold_kernel, out_shape=jax.ShapeDtypeStruct((windows, memb...  4.63 us

profile of v1, /device:TPU:0, one launch (start us, length us, event | category | flops | bytes accessed | tf_op | source)
XLA Modules:
  0.0 108.2 jit_solution(12854475997944051353)
XLA Ops:
  0.0 0.7 fusion.4
  0.7 0.1 reshape.8
  0.8 0.8 select_bitcast_fusion
  1.5 13.6 %all-gather.1 = f32[4,32,3]{1,2,0:T(4,128)S(1)} all-gather(f32[1,32,3]{1,2,0:T(4,128)S(1)} %select_bitcast_fusion), channel_id=1, replica_groups=mesh['tm'=8,'cell'=4] {'cell'}, dimensions={0}, use_global_device_ids=true | all-gather | bytes 1920 | tf_op jit(solution)/shard_map/all_gather | solution.py:160
  15.2 0.1 reshape.21
  15.2 0.8 copy.21.weight_ref
  16.1 2.1 %slice_bitcast_fusion = bf16[3,2048,256]{2,1,0:T(8,128)(2,1)S(1)} fusion(bf16[3,2,2048,256]{3,2,1,0:T(8,128)(2,1)} %param.5), kind=kLoop, calls=%fused_computation.3 | loop fusion | bytes 6291456 | tf_op jit(solution)/shard_map/vmap()/squeeze | solution.py:156
  18.2 1.5 %gather_fusion = bf16[96,256]{1,0:T(8,128)(2,1)S(1)} fusion(bf16[3,2048,256]{2,1,0:T(8,128)(2,1)S(1)} %slice_bitcast_fusion, s32[96]{0:T(128)S(1)} %reshape.8), kind=kCustom, calls=%fused_computation | custom fusion | bytes 99072 | tf_op jit(solution)/shard_map/vmap()/gather | solution.py:156
  19.6 14.6 %all_gather.12.picked_ref = bf16[3,128,256]{2,1,0:T(8,128)(2,1)} all-gather(bf16[3,32,256]{2,1,0:T(8,128)(2,1)S(1)} %bitcast.31), channel_id=1, replica_groups=mesh['tm'=8,'cell'=4] {'cell'}, dimensions={1}, use_global_device_ids=true | all-gather | bytes 245760 | tf_op jit(solution)/shard_map/all_gather | solution.py:159
  34.3 40.8 %transforms.1 = (f32[3,256,256]{2,1,0:T(8,128)}, bf16[3,128,128]{2,1,0:T(8,128)(2,1)}) custom-call(f32[3]{0:T(128)} %rho_ref.1, bf16[3,128,256]{2,1,0:T(8,128)(2,1)} %all_gather.12.picked_ref, f32[3,128,1]{2,1,0:T(8,128)} %copy.21.weight_ref), custom_call_target="tpu_custom_call" | custom-call | tf_op jit(solution)/shard_map/transforms/pallas_call | solution.py:163
  75.1 12.5 %all-gather = bf16[24,128,128]{2,1,0:T(8,128)(2,1)} all-gather(bf16[3,128,128]{2,1,0:T(8,128)(2,1)} %get-tuple-element.7), channel_id=2, replica_groups=mesh['tm'=8,'cell'=4] {'tm'}, dimensions={0}, use_global_device_ids=true | all-gather | bytes 884736 | tf_op jit(solution)/shard_map/all_gather | solution.py:175
  87.5 4.6 %fold.1 = bf16[3,256,256]{2,1,0:T(8,128)(2,1)} custom-call(s32[1]{0:T(128)} %bitcast.position_ref, bf16[8,3,128,128]{3,2,1,0:T(8,128)(2,1)} %bitcast.30, f32[3,256,256]{2,1,0:T(8,128)} %get-tuple-element.8.partial_ref), custom_call_target="tpu_custom_call" | custom-call | tf_op jit(solution)/shard_map/fold/pallas_call | solution.py:176
  92.2 7.4 %fusion = bf16[3,4096,256]{1,2,0:T(8,128)(2,1)} fusion(bf16[3,256,256]{2,1,0:T(8,128)(2,1)} %fold.1, bf16[3,4096,256]{2,1,0:T(8,128)(2,1)} %bitcast.29), kind=kOutput, calls=%fused_computation.2 | convolution fusion | flops 1613758464 | bytes 12976128 | tf_op jit(solution)/shard_map/wcm,wmn->wcn/dot_general | solution.py:185
  99.6 8.6 %copy.25 = bf16[3,4096,256]{2,1,0:T(8,128)(2,1)} copy(bf16[3,4096,256]{1,2,0:T(8,128)(2,1)} %fusion) | data formatting | bytes 12582912 | tf_op jit(solution)/shard_map/reshape | solution.py:186
  (1 shorter events, 0.0 us)

commit v2 on v1

--- a/solution.py
+++ b/solution.py
@@ -36,25 +36,37 @@
     lane = lax.broadcasted_iota(jnp.int32, (8, size), 1)
     sub = lax.broadcasted_iota(jnp.int32, (8, size), 0)
     work = [[m[8 * g : 8 * g + 8, :] for g in range(groups)] for m in matrices]
-    for k in range(size):
+    for k in range(0, size, 2):
         g, r = divmod(k, 8)
-        at_k = lane == k
-        below = sub > r
+        first_lane, second_lane = lane == k, lane == k + 1
+        either = first_lane | second_lane
         for rows in work:
             own = rows[g]
-            pivot_row = jnp.broadcast_to(own[r : r + 1, :], (8, size))
-            inverse = 1.0 / own[r : r + 1, k : k + 1]
-            scaled = jnp.where(at_k, 1.0, pivot_row) * inverse
+            near = jnp.broadcast_to(own[:, k : k + 1], (8, size))
+            far = jnp.broadcast_to(own[:, k + 1 : k + 2], (8, size))
+            d0 = jnp.broadcast_to(near[r : r + 1, :], (8, size))
+            m = jnp.broadcast_to(near[r + 1 : r + 2, :], (8, size))
+            e = jnp.broadcast_to(far[r + 1 : r + 2, :], (8, size))
+            row0 = jnp.broadcast_to(own[r : r + 1, :], (8, size))
+            row1 = jnp.broadcast_to(own[r + 1 : r + 2, :], (8, size))
+            i0 = 1.0 / d0
+            step = m * i0
+            i1 = 1.0 / (e - step * m)
+            row0_one = jnp.where(first_lane, 1.0, row0)
+            row1_mid = jnp.where(first_lane, 0.0, row1) - step * row0_one
+            p0 = jnp.where(second_lane, 0.0, row0_one) * i0
+            p1 = jnp.where(second_lane, 1.0, row1_mid) * i1
             for i in range(g, groups):
-                column = jnp.broadcast_to(rows[i][:, k : k + 1], (8, size))
                 if i == g:
-                    if r == 7:
-                        continue
-                    column = jnp.where(below, column, 0.0)
-                    base = jnp.where(at_k & below, 0.0, rows[i])
+                    c0, c1 = near, far
                 else:
-                    base = jnp.where(at_k, 0.0, rows[i])
-                rows[i] = base - column * scaled
+                    c0 = jnp.broadcast_to(rows[i][:, k : k + 1], (8, size))
+                    c1 = jnp.broadcast_to(rows[i][:, k + 1 : k + 2], (8, size))
+                c1 = c1 - c0 * step
+                new = jnp.where(either, 0.0, rows[i]) - c0 * p0 - c1 * p1
+                if i == g:
+                    new = jnp.where(sub <= r, own, jnp.where(sub == r + 1, row1_mid, new))
+                rows[i] = new
     results = []
     for rows in work:
         pieces = []
@@ -70,9 +82,12 @@
 def transforms_kernel(
     rho_ref, picked_ref, weight_ref, partial_ref, own_ref, gram, first_inv, second_inv, low_ref, mid_ref
 ):
-    windows = picked_ref.shape[0]
-    members = picked_ref.shape[2]
+    blocks, windows, slots, members = picked_ref.shape
     half = members // 2
+    slot_eye = (
+        lax.broadcasted_iota(jnp.int32, (slots, slots), 0)
+        == lax.broadcasted_iota(jnp.int32, (slots, slots), 1)
+    )
     eye = (
         lax.broadcasted_iota(jnp.int32, (members, members), 0)
         == lax.broadcasted_iota(jnp.int32, (members, members), 1)
@@ -82,8 +97,14 @@
 
     @pl.loop(0, windows)
     def _(w):
-        rows = picked_ref[w]
-        high, low = halves(rows.astype(F32) * weight_ref[w])
+        rows = jnp.concatenate([picked_ref[n, w] for n in range(blocks)], axis=0)
+        columns = [
+            jnp.sum(
+                jnp.where(slot_eye, weight_ref[n, pl.ds(w, 1), :], 0.0), axis=1, keepdims=True
+            )
+            for n in range(blocks)
+        ]
+        high, low = halves(rows.astype(F32) * jnp.concatenate(columns, axis=0))
         total = dot_any(high, rows, tn) + dot_any(low, rows, tn)
         gram[w] = total + jnp.where(eye, F32(members - 1.0), 0.0)
 
@@ -147,6 +168,71 @@
         out_ref[w] = dot_three(partial_ref[w], later[...]).astype(BF16)
 
 
+def exchange_kernel(axis, count, one_way, items, *refs):
+    ins, outs = refs[:items], refs[items : 2 * items]
+    send_sem, recv_sem = refs[2 * items :]
+    me = lax.axis_index(axis)
+    barrier = pltpu.get_barrier_semaphore()
+    for shift in range(1, count):
+        pl.semaphore_signal(
+            barrier,
+            inc=1,
+            device_id={axis: lax.rem(me + shift, count)},
+            device_id_type=pl.DeviceIdType.MESH,
+        )
+    pl.semaphore_wait(barrier, count - 1)
+
+    def copy_of(shift, item):
+        return pltpu.make_async_remote_copy(
+            src_ref=ins[item],
+            dst_ref=outs[item].at[me],
+            send_sem=send_sem.at[item, shift],
+            recv_sem=recv_sem.at[item, shift],
+            device_id={axis: lax.rem(me + count - shift, count)},
+            device_id_type=pl.DeviceIdType.MESH,
+        )
+
+    def when(condition, action):
+        if one_way:
+            pl.when(condition)(action)
+        else:
+            action()
+
+    order = [(shift, item) for shift in range(1, count) for item in range(items)]
+    for shift, item in order:
+        when(me >= shift, lambda: copy_of(shift, item).start())
+    if not one_way:
+        for item in range(items):
+            outs[item][me] = ins[item][...]
+    for shift, item in order:
+        when(me >= shift, lambda: copy_of(shift, item).wait_send())
+        when(me + shift < count, lambda: copy_of(shift, item).wait_recv())
+
+
+def exchange(axis, one_way, collective_id, *values):
+    count = lax.axis_size(axis)
+    items = len(values)
+    vmem = pl.BlockSpec(memory_space=pltpu.VMEM)
+    return pl.pallas_call(
+        lambda *refs: exchange_kernel(axis, count, one_way, items, *refs),
+        out_shape=tuple(jax.ShapeDtypeStruct((count,) + v.shape, v.dtype) for v in values),
+        in_specs=[vmem] * items,
+        out_specs=(vmem,) * items,
+        scratch_shapes=[
+            pltpu.SemaphoreType.DMA((items, count)),
+            pltpu.SemaphoreType.DMA((items, count)),
+        ],
+        compiler_params=pltpu.CompilerParams(collective_id=collective_id, has_side_effects=True),
+        name="exchange_" + axis,
+    )(*values)
+
+
+def apply_kernel(field_ref, weight_ref, out_ref):
+    out_ref[0] = jnp.dot(field_ref[0], weight_ref[0], preferred_element_type=F32).astype(
+        out_ref.dtype
+    )
+
+
 def local(anomalies, obs_cells, obs_counts, obs_precision, inflation):
     windows, _, cell_width, members = anomalies.shape
     half = members // 2
@@ -156,8 +242,7 @@
     picked = jax.vmap(lambda field, where_at: field[0][where_at])(anomalies, offsets)
     live = jnp.arange(slots, dtype=jnp.int32)[None, :] < obs_counts
     weights = jnp.where(live, obs_precision, jnp.float32(0.0))
-    gathered = lax.all_gather(picked, "cell", axis=1, tiled=True)
-    gathered_weights = lax.all_gather(weights, "cell", axis=1, tiled=True)
+    gathered, gathered_weights = exchange("cell", False, 0, picked, weights)
     vmem = pl.BlockSpec(memory_space=pltpu.VMEM)
     smem = pl.BlockSpec(memory_space=pltpu.SMEM)
     partial, own = pl.pallas_call(
@@ -171,8 +256,8 @@
         scratch_shapes=[pltpu.VMEM((windows, members, members), F32)]
         + [pltpu.VMEM((windows, half, half), F32)] * 4,
         name="transforms",
-    )(inflation, gathered, gathered_weights[:, :, None])
-    products = lax.all_gather(own, "tm", axis=0)
+    )(inflation, gathered, gathered_weights)
+    (products,) = exchange("tm", True, 1, own)
     weight_mats = pl.pallas_call(
         fold_kernel,
         out_shape=jax.ShapeDtypeStruct((windows, members, members), BF16),
@@ -182,8 +267,19 @@
         name="fold",
     )(lax.axis_index("tm").astype(jnp.int32)[None], products, partial)
     flat = anomalies.reshape(windows, 2 * cell_width, members)
-    result = jnp.einsum("wcm,wmn->wcn", flat, weight_mats, preferred_element_type=jnp.float32)
-    return result.astype(jnp.bfloat16).reshape(anomalies.shape)
+    tile = min(2048, 2 * cell_width)
+    result = pl.pallas_call(
+        apply_kernel,
+        out_shape=jax.ShapeDtypeStruct(flat.shape, BF16),
+        grid=(windows, 2 * cell_width // tile),
+        in_specs=[
+            pl.BlockSpec((1, tile, members), lambda w, c: (w, c, 0)),
+            pl.BlockSpec((1, members, members), lambda w, c: (w, 0, 0)),
+        ],
+        out_specs=pl.BlockSpec((1, tile, members), lambda w, c: (w, c, 0)),
+        name="apply",
+    )(flat, weight_mats)
+    return result.reshape(anomalies.shape)
 
 
 def solution(mesh):

time: 109 us -> 71.9 us (0.66)
  blocking collectives: 40.7 us -> 0 us
  Pallas kernels: 45.4 us -> 65.1 us
  local copies, waits for them, and re-layouts: 13.2 us -> 4.34 us
  matrix products: 7.44 us -> 0 us
    all_gather x3 -> x0, blocking collectives: 40.7 us -> none  [the longest x1 14.6 us: local(): gathered = lax.all_gather(picked, 'cell', axis=1, tiled=True)]
    pallas_call x0 -> x3, Pallas kernels: none -> 34.4 us  [the longest x2 26.3 us: exchange(): pl.pallas_call(lambda *refs: exchange_kernel(axis, count, one_way, items,...]
    pallas_call x1, Pallas kernels: 40.8 us -> 26.1 us  [local(): pl.pallas_call(transforms_kernel, out_shape=(jax.ShapeDtypeStruct((window...]
    reshape x1 -> x0, local copies, waits for them, and re-layouts: 8.6 us -> none  [local(): return result.astype(jnp.bfloat16).reshape(anomalies.shape)]
    dot_general x1 -> x0, matrix products: 7.44 us -> none  [local(): jnp.einsum('wcm,wmn->wcn', flat, weight_mats, preferred_element_type=jnp....]
    select_n x0 -> x1, other arithmetic: none -> 1.33 us  [local(): weights = jnp.where(live, obs_precision, jnp.float32(0.0))]
where the time goes in v2:
time: 71.9 us; the launch traced here: 71.5 us
  Pallas kernels  65.1 us (91%)
  local copies, waits for them, and re-layouts  4.34 us (6%)
  other arithmetic  2.02 us (3%)
    pallas_call x2, Pallas kernels, exchange(): pl.pallas_call(lambda *refs: exchange_kernel(axis, count, one_way, items,...  26.3 us
    pallas_call x1, Pallas kernels, local(): pl.pallas_call(transforms_kernel, out_shape=(jax.ShapeDtypeStruct((window...  26.1 us
    pallas_call x1, Pallas kernels, local(): pl.pallas_call(apply_kernel, out_shape=jax.ShapeDtypeStruct(flat.shape, B...  8.01 us
    pallas_call x1, Pallas kernels, local(): pl.pallas_call(fold_kernel, out_shape=jax.ShapeDtypeStruct((windows, memb...  4.61 us
    gather x2, local copies, waits for them, and re-layouts, local(): field[0][where_at]  2.24 us
    squeeze x1, local copies, waits for them, and re-layouts, local(): field[0][where_at]  2.09 us

profile of v2, /device:TPU:0, one launch (start us, length us, event | category | flops | bytes accessed | tf_op | source)
XLA Modules:
  0.0 71.5 jit_solution(10637145085186539722)
XLA Ops:
  0.0 0.7 fusion.3
  0.7 0.1 reshape.8
  0.8 1.3 %fusion.4.refs_1_ = f32[3,32]{1,0:T(4,128)} fusion(f32[3,32]{1,0:T(4,128)} %param.8, s32[3]{0:T(128)} %bitcast.17), kind=kLoop, calls=%fused_computation.8 | loop fusion | flops 192 | bytes 780 | tf_op jit(solution)/shard_map/jit(_where)/select_n | solution.py:244
  2.1 2.1 %slice_bitcast_fusion = bf16[3,2048,256]{2,1,0:T(8,128)(2,1)S(1)} fusion(bf16[3,2,2048,256]{3,2,1,0:T(8,128)(2,1)} %param.5), kind=kLoop, calls=%fused_computation.1 | loop fusion | bytes 6291456 | tf_op jit(solution)/shard_map/vmap()/squeeze | solution.py:242
  4.2 2.2 %gather_fusion = bf16[96,256]{1,0:T(8,128)(2,1)} fusion(bf16[3,2048,256]{2,1,0:T(8,128)(2,1)S(1)} %slice_bitcast_fusion, s32[96]{0:T(128)S(1)} %reshape.8), kind=kCustom, calls=%fused_computation | custom fusion | bytes 99072 | tf_op jit(solution)/shard_map/vmap()/gather | solution.py:242
  6.4 12.0 %exchange_cell.1 = (bf16[4,3,32,256]{3,2,1,0:T(8,128)(2,1)}, f32[4,3,32]{2,1,0:T(4,128)}) custom-call(bf16[3,32,256]{2,1,0:T(8,128)(2,1)} %bitcast.16, f32[3,32]{1,0:T(4,128)} %fusion.4.refs_1_), custom_call_target="tpu_custom_call" | custom-call | tf_op jit(solution)/shard_map/exchange_cell/pallas_call | solution.py:216
  18.4 26.1 %transforms.1 = (f32[3,256,256]{2,1,0:T(8,128)}, bf16[3,128,128]{2,1,0:T(8,128)(2,1)}) custom-call(f32[3]{0:T(128)} %rho_ref.1, bf16[4,3,32,256]{3,2,1,0:T(8,128)(2,1)} %get-tuple-element.9.picked_ref, f32[4,3,32]{2,1,0:T(4,128)} %get-tuple-element.10.weight_ref), custom_call_target="tpu_custom_call" | custom-call | tf_op jit(solution)/shard_map/transforms/pallas_call | solution.py:248
  44.5 14.3 %exchange_tm.1.products_ref = bf16[8,3,128,128]{3,2,1,0:T(8,128)(2,1)} custom-call(bf16[3,128,128]{2,1,0:T(8,128)(2,1)} %get-tuple-element.11.refs_0_), custom_call_target="tpu_custom_call" | custom-call | tf_op jit(solution)/shard_map/exchange_tm/pallas_call | solution.py:216
  58.8 4.6 %fold.1.weight_ref = bf16[3,256,256]{2,1,0:T(8,128)(2,1)} custom-call(s32[1]{0:T(128)} %bitcast.1.position_ref, bf16[8,3,128,128]{3,2,1,0:T(8,128)(2,1)} %exchange_tm.1.products_ref, f32[3,256,256]{2,1,0:T(8,128)} %get-tuple-element.12.partial_ref), custom_call_target="tpu_custom_call" | custom-call | tf_op jit(solution)/shard_map/fold/pallas_call | solution.py:261
  63.4 8.0 %apply.1 = bf16[3,4096,256]{2,1,0:T(8,128)(2,1)} custom-call(bf16[3,4096,256]{2,1,0:T(8,128)(2,1)} %bitcast.15, bf16[3,256,256]{2,1,0:T(8,128)(2,1)} %fold.1.weight_ref), custom_call_target="tpu_custom_call" | custom-call | tf_op jit(solution)/shard_map/apply/pallas_call | solution.py:271
